TPU v7x, 32 devices: a whole 2x2x4 slice. The times are simulated.
32 devices in a mesh: rep: 2 (over x), dp: 16 (over y, z, core).
Axes of the slice: x: 2, y: 2, z: 4, core: 2. Of those that a mesh axis runs over, the one named last changes fastest.
Arguments:
- x: bfloat16 [32, 1024, 512], P(('rep', 'dp')), parts along dimension 0
- dy: bfloat16 [32, 1024, 512], P(('rep', 'dp')), parts along dimension 0
- w_gate: bfloat16 [2, 512, 8192], P(None, 'dp')
- w_up: bfloat16 [2, 512, 8192], P(None, 'dp')
- w_down: bfloat16 [2, 8192, 512], P(None, 'dp')
- m_w_gate: float32 [2, 512, 8192], P(None, 'dp')
- m_w_up: float32 [2, 512, 8192], P(None, 'dp')
- m_w_down: float32 [2, 8192, 512], P(None, 'dp')
- v_w_gate: float32 [2, 512, 8192], P(None, 'dp')
- v_w_up: float32 [2, 512, 8192], P(None, 'dp')
- v_w_down: float32 [2, 8192, 512], P(None, 'dp')
Outputs:
- output 1: bfloat16 [4, 512, 8192], P('rep', 'dp'), parts along dimension 0
- output 2: bfloat16 [4, 512, 8192], P('rep', 'dp'), parts along dimension 0
- output 3: bfloat16 [4, 8192, 512], P('rep', 'dp'), parts along dimension 0
- output 4: float32 [4, 512, 8192], P('rep', 'dp'), parts along dimension 0
- output 5: float32 [4, 512, 8192], P('rep', 'dp'), parts along dimension 0
- output 6: float32 [4, 8192, 512], P('rep', 'dp'), parts along dimension 0
- output 7: float32 [4, 512, 8192], P('rep', 'dp'), parts along dimension 0
- output 8: float32 [4, 512, 8192], P('rep', 'dp'), parts along dimension 0
- output 9: float32 [4, 8192, 512], P('rep', 'dp'), parts along dimension 0
There are 2 independent parts. A program takes and returns all parts, laid end to end along the dimension named above; an argument that names none is the same for every part.
All inputs are finite; a program needn't handle non-finite values.
Results may differ from a plain program's by a relative error of at most 0.022.
Values are sent between devices in bfloat16 or wider.
A program may use at most 2 GiB of HBM per device.

v0:
```python
import jax
import jax.numpy as jnp
from jax import lax
from jax.sharding import PartitionSpec as P

NAMES = ("w_gate", "w_up", "w_down")


def matmul(a, w):
    return jnp.dot(a, w, preferred_element_type=jnp.float32).astype(jnp.bfloat16)


def normed(h):
    wide = h.astype(jnp.float32)
    scale = lax.rsqrt(jnp.mean(wide**2, -1, keepdims=True) + 1e-6)
    return (wide * scale).astype(jnp.bfloat16)


def layer(h, w):
    a = normed(h)
    gate = jnp.dot(a, w["w_gate"], preferred_element_type=jnp.float32)
    up = jnp.dot(a, w["w_up"], preferred_element_type=jnp.float32)
    return h + matmul((jax.nn.silu(gate) * up).astype(jnp.bfloat16), w["w_down"])


def adamw(w, m, v, g):
    m = 0.9 * m + 0.1 * g
    v = 0.95 * v + 0.05 * g * g
    step = m * lax.rsqrt(v + 1e-8) + 0.1 * w
    return (w - 0.02 * step).astype(jnp.bfloat16), m, v


def clipped(gradients, sum_of_squares, count):
    factor = jnp.minimum(1.0, 0.5 * lax.rsqrt(sum_of_squares / count + 1e-30))
    return [g * factor for g in gradients]


def solution(mesh):
    def fetched(weights, number):
        return {name: lax.all_gather(w[number], "dp", axis=0, tiled=True) for name, w in zip(NAMES, weights, strict=True)}

    def step(x, dy, *arrays):
        weights, m, v = (arrays[i : i + 3] for i in (0, 3, 6))
        layers = weights[0].shape[0]
        h, kept = x[0], []
        for number in range(layers):
            kept.append(h)
            h = layer(h, fetched(weights, number))
        by_h, mine = dy[0], [None] * layers
        for number in reversed(range(layers)):
            _, back = jax.vjp(lambda w, h: layer(h, w), fetched(weights, number), kept[number])
            by_w, by_h = back(by_h)
            mine[number] = [lax.psum_scatter(by_w[name], "dp", scatter_dimension=0, tiled=True) for name in NAMES]
        gradients = [jnp.stack([mine[number][i] for number in range(layers)]).astype(jnp.float32) for i in range(3)]
        squares = lax.psum(sum(jnp.sum(g * g) for g in gradients), "dp")
        gradients = clipped(gradients, squares, lax.psum(1, "dp") * sum(g.size for g in gradients))
        new = [adamw(w.astype(jnp.float32), m, v, g) for w, m, v, g in zip(weights, m, v, gradients, strict=True)]
        return tuple(one[which] for which in range(3) for one in new)

    states, cut = P(("rep", "dp"), None, None), P(None, "dp", None)
    return jax.shard_map(
        step,
        mesh=mesh,
        in_specs=(states, states) + (cut,) * 9,
        out_specs=(P("rep", "dp", None),) * 9,
        check_vma=False,
    )
```

profile of v0, /device:TPU:0, one launch (start us, length us, event | category | flops | bytes accessed | tf_op | source)
XLA Modules:
  0.0 1250.9 jit_solution(15872639961188315696)
XLA Ops:
  7.2 2.4 fusion.105
  9.7 2.2 fusion.104
  12.0 2.2 fusion.103
  14.3 0.5 all-gather.21.cloned.1.call-update
  14.9 0.5 all-gather.23.cloned.1.call-update
  15.5 0.5 all-gather.19.cloned.1.call-update
  16.1 0.5 copy.20
  16.6 0.2 fusion.46
  16.9 1.3 copy.21
  18.2 69.9 %all-gather.13.cloned.1.call-done = bf16[1,512,8192]{2,1,0:T(8,128)(2,1)} async-done(((bf16[1,32,8192]{2,1,0:T(8,128)(2,1)}), bf16[1,512,8192]{2,1,0:T(8,128)(2,1)}) %all-gather.13.cloned.1.call-update) | async-done | bytes 8388624 | tf_op jit(solution)/shard_map/all_gather | solution.py:40
  88.1 18.7 %fusion.34 = f32[1024,8192]{1,0:T(8,128)} fusion(bf16[1,512,8192]{2,1,0:T(8,128)(2,1)} %all-gather.13.cloned.1.call-done, bf16[1,1024,512]{1,2,0:T(8,128)(2,1)S(1)} %copy.20, f32[1024]{0:T(1024)S(1)} %add_rsqrt_fusion), kind=kOutput, calls=%fused_computation.45 | convolution fusion | flops 8591507456 | bytes 42995712 | tf_op jit(solution)/shard_map/dot_general | solution.py:21
  106.8 56.8 %all-gather.15.cloned.1.call-done = bf16[1,512,8192]{2,1,0:T(8,128)(2,1)} async-done(((bf16[1,32,8192]{2,1,0:T(8,128)(2,1)}), bf16[1,512,8192]{2,1,0:T(8,128)(2,1)}) %all-gather.15.cloned.1.call-update) | async-done | bytes 8388624 | tf_op jit(solution)/shard_map/all_gather | solution.py:40
  163.6 33.2 %multiply_convert_fusion.1 = (bf16[1024,8192]{1,0:T(8,128)(2,1)}, f32[1024,8192]{1,0:T(8,128)}) fusion(f32[1024,8192]{1,0:T(8,128)} %fusion.34, bf16[1,512,8192]{2,1,0:T(8,128)(2,1)} %all-gather.15.cloned.1.call-done, bf16[1,1024,512]{1,2,0:T(8,128)(2,1)S(1)} %copy.20, f32[1024]{0:T(1024)S(1)} %add_rsqrt_fusion), kind=kOutput, calls=%fused_computation.17 | convolution fusion | flops 8641839104 | bytes 93327360 | tf_op jit(solution)/shard_map/dot_general | solution.py:22
  196.8 42.3 %all-gather.17.cloned.1.call-done = bf16[1,8192,512]{2,1,0:T(8,128)(2,1)} async-done(((bf16[1,512,512]{2,1,0:T(8,128)(2,1)}), bf16[1,8192,512]{2,1,0:T(8,128)(2,1)}) %all-gather.17.cloned.1.call-update) | async-done | bytes 8388624 | tf_op jit(solution)/shard_map/all_gather | solution.py:40
  239.2 15.1 %fusion.62 = (f32[1024]{0:T(1024)S(1)}, bf16[1024,512]{0,1:T(8,128)(2,1)S(1)}) fusion(bf16[1024,8192]{1,0:T(8,128)(2,1)} %get-tuple-element.24, bf16[1,8192,512]{2,1,0:T(8,128)(2,1)} %all-gather.17.cloned.1.call-done, bf16[1,1024,512]{1,2,0:T(8,128)(2,1)S(1)} %copy.20), kind=kOutput, calls=%fused_computation.94 | convolution fusion | flops 8592555008 | bytes 27267072 | tf_op jit(solution)/shard_map/dot_general | solution.py:10
  254.3 60.2 %all-gather.21.cloned.1.call-done = bf16[1,8192,512]{2,1,0:T(8,128)(2,1)} async-done(((bf16[1,512,512]{2,1,0:T(8,128)(2,1)}), bf16[1,8192,512]{2,1,0:T(8,128)(2,1)}) %all-gather.21.cloned.1.call-update) | async-done | bytes 8388624 | tf_op jit(solution)/shard_map/all_gather | solution.py:40
  314.5 15.1 %convolution_convert_fusion.1 = bf16[1024,8192]{1,0:T(8,128)(2,1)} fusion(bf16[1,8192,512]{2,1,0:T(8,128)(2,1)} %all-gather.21.cloned.1.call-done, bf16[1,1024,512]{2,1,0:T(8,128)(2,1)S(1)} %copy-done.17), kind=kOutput, calls=%fused_computation.25 | convolution fusion | flops 8598323200 | bytes 26214400 | tf_op jit(solution)/shard_map/transpose(jvp())/dot_general | solution.py:10
  329.7 60.2 %all-gather.23.cloned.1.call-done = bf16[1,512,8192]{2,1,0:T(8,128)(2,1)} async-done(((bf16[1,32,8192]{2,1,0:T(8,128)(2,1)}), bf16[1,512,8192]{2,1,0:T(8,128)(2,1)}) %all-gather.23.cloned.1.call-update) | async-done | bytes 8388624 | tf_op jit(solution)/shard_map/all_gather | solution.py:40
  389.9 18.7 %fusion.21 = f32[1024,8192]{1,0:T(8,128)} fusion(bf16[1,512,8192]{2,1,0:T(8,128)(2,1)} %all-gather.23.cloned.1.call-done, bf16[1024,512]{0,1:T(8,128)(2,1)S(1)} %get-tuple-element.27, f32[1024]{0:T(1024)S(1)} %fusion.91), kind=kOutput, calls=%fused_computation.32 | convolution fusion | flops 8591507456 | bytes 42995712 | tf_op jit(solution)/shard_map/jvp()/dot_general | solution.py:22
  408.6 56.7 %all-gather.19.cloned.1.call-done = bf16[1,512,8192]{2,1,0:T(8,128)(2,1)} async-done(((bf16[1,32,8192]{2,1,0:T(8,128)(2,1)}), bf16[1,512,8192]{2,1,0:T(8,128)(2,1)}) %all-gather.19.cloned.1.call-update) | async-done | bytes 8388624 | tf_op jit(solution)/shard_map/all_gather | solution.py:40
  465.3 41.1 %fusion.2 = (bf16[1024,8192]{1,0:T(8,128)(2,1)}, f32[1024,8192]{1,0:T(8,128)}) fusion(f32[1024,8192]{1,0:T(8,128)} %fusion.21, bf16[1024,8192]{1,0:T(8,128)(2,1)} %convolution_convert_fusion.1, bf16[1,512,8192]{2,1,0:T(8,128)(2,1)} %all-gather.19.cloned.1.call-done, bf16[1024,512]{0,1:T(8,128)(2,1)S(1)} %get-tuple-element.27, f32[1024]{0:T(1024)S(1)} %fusion.91), kind=kOutput, calls=%fused_computation.8 | convolution fusion | flops 8692170752 | bytes 110104576 | tf_op jit(solution)/shard_map/jvp()/dot_general | solution.py:21
  506.3 21.1 %fusion.71 = bf16[1024,512]{0,1:T(8,128)(2,1)S(1)} fusion(bf16[1,512,8192]{2,1,0:T(8,128)(2,1)} %all-gather.23.cloned.1.call-done, bf16[1024,8192]{1,0:T(8,128)(2,1)} %convolution_convert_fusion.1, f32[1024,8192]{1,0:T(8,128)} %get-tuple-element.29), kind=kOutput, calls=%fused_computation.99 | convolution fusion | flops 8640790528 | bytes 59768832 | tf_op jit(solution)/shard_map/transpose(jvp())/dot_general | solution.py:22
  527.5 12.8 %fusion.64 = (f32[1024]{0:T(1024)S(1)}, bf16[1024,512]{0,1:T(8,128)(2,1)S(1)}) fusion(bf16[1024,512]{0,1:T(8,128)(2,1)S(1)} %get-tuple-element.27, bf16[1024,512]{0,1:T(8,128)(2,1)S(1)} %fusion.71, bf16[1024,8192]{1,0:T(8,128)(2,1)} %get-tuple-element.28, bf16[1,512,8192]{2,1,0:T(8,128)(2,1)S(1)} %copy-done.25), kind=kOutput, calls=%fused_computation.96 | convolution fusion | flops 8592555008 | bytes 28315648 | tf_op jit(solution)/shard_map/transpose(jvp())/dot_general | solution.py:21
  540.4 0.7 fusion.80
  541.1 17.4 %convolution_convert_fusion.2 = bf16[8192,512]{1,0:T(8,128)(2,1)} fusion(bf16[1024,8192]{1,0:T(8,128)(2,1)} %get-tuple-element.24, bf16[1024,512]{0,1:T(8,128)(2,1)S(1)} %fusion.80), kind=kOutput, calls=%fused_computation.30 | convolution fusion | flops 8594128896 | bytes 26214400 | tf_op jit(solution)/shard_map/transpose(jvp())/dot_general | solution.py:10
  558.6 1.2 copy-done.18
  559.7 26.8 %fusion.18 = bf16[8192,512]{1,0:T(8,128)(2,1)} fusion(f32[1024,8192]{1,0:T(8,128)} %fusion.21, bf16[1,1024,512]{2,1,0:T(8,128)(2,1)S(1)} %copy-done.18, f32[1024,8192]{1,0:T(8,128)} %get-tuple-element.29), kind=kOutput, calls=%fused_computation.27 | convolution fusion | flops 8644460544 | bytes 76546048 | tf_op jit(solution)/shard_map/transpose(jvp())/dot_general | solution.py:10
  586.6 16.1 %convolution_convert_fusion = bf16[1024,8192]{1,0:T(8,128)(2,1)} fusion(bf16[1024,512]{0,1:T(8,128)(2,1)S(1)} %fusion.80, bf16[1,8192,512]{2,1,0:T(8,128)(2,1)} %all-gather.17.cloned.1.call-done), kind=kOutput, calls=%fused_computation.24 | convolution fusion | flops 8598323200 | bytes 26214400 | tf_op jit(solution)/shard_map/transpose(jvp())/dot_general | solution.py:10
  602.7 22.3 %fusion.20 = bf16[512,8192]{1,0:T(8,128)(2,1)} fusion(bf16[1024,8192]{1,0:T(8,128)(2,1)} %convolution_convert_fusion, f32[1024,8192]{1,0:T(8,128)} %fusion.34, bf16[1,1024,512]{1,2,0:T(8,128)(2,1)S(1)} %copy-done.1, f32[1024]{0:T(1024)S(1)} %copy-done.22), kind=kOutput, calls=%fused_computation.29 | convolution fusion | flops 8646033408 | bytes 59772928 | tf_op jit(solution)/shard_map/transpose(jvp())/dot_general | solution.py:22
  625.0 1.1 copy-done.6
  626.2 22.5 %fusion.19 = bf16[512,8192]{1,0:T(8,128)(2,1)} fusion(bf16[1024,8192]{1,0:T(8,128)(2,1)} %convolution_convert_fusion.1, bf16[1024,512]{0,1:T(8,128)(2,1)S(1)} %copy-done.6, f32[1024]{0:T(1024)S(1)} %copy-done.20, f32[1024,8192]{1,0:T(8,128)} %get-tuple-element.29), kind=kOutput, calls=%fused_computation.28 | convolution fusion | flops 8646033408 | bytes 59772928 | tf_op jit(solution)/shard_map/transpose(jvp())/dot_general | solution.py:22
  648.7 32.9 %fusion.15 = bf16[512,8192]{1,0:T(8,128)(2,1)} fusion(f32[1024,8192]{1,0:T(8,128)} %fusion.34, f32[1024,8192]{1,0:T(8,128)} %get-tuple-element.25, bf16[1024,8192]{1,0:T(8,128)(2,1)} %convolution_convert_fusion, bf16[1,1024,512]{1,2,0:T(8,128)(2,1)S(1)} %copy-done.1, f32[1024]{0:T(1024)S(1)} %copy-done.22), kind=kOutput, calls=%fused_computation.26 | convolution fusion | flops 8687976448 | bytes 93327360 | tf_op jit(solution)/shard_map/transpose(jvp())/dot_general | solution.py:21
  681.8 17.1 %convolution_convert_fusion.3 = bf16[512,8192]{1,0:T(8,128)(2,1)} fusion(bf16[1024,8192]{1,0:T(8,128)(2,1)} %get-tuple-element.28, bf16[1024,512]{0,1:T(8,128)(2,1)S(1)} %copy-done.6, f32[1024]{0:T(1024)S(1)} %copy-done.20), kind=kOutput, calls=%fused_computation.31 | convolution fusion | flops 8591507456 | bytes 26218496 | tf_op jit(solution)/shard_map/transpose(jvp())/dot_general | solution.py:21
  699.0 68.0 %reduce-scatter.17.cloned.1.call-done = bf16[512,512]{1,0:T(8,128)(2,1)} async-done(((bf16[8192,512]{1,0:T(8,128)(2,1)}), bf16[512,512]{1,0:T(8,128)(2,1)}) %reduce-scatter.17.cloned.1.call-update) | async-done | bytes 524304 | tf_op jit(solution)/shard_map/reduce_scatter | solution.py:53
  767.0 2.3 fusion.52
  769.3 104.5 %reduce-scatter.11.cloned.1.call-done = bf16[32,8192]{1,0:T(8,128)(2,1)} async-done(((bf16[512,8192]{1,0:T(8,128)(2,1)}), bf16[32,8192]{1,0:T(8,128)(2,1)}) %reduce-scatter.11.cloned.1.call-update) | async-done | bytes 524304 | tf_op jit(solution)/shard_map/reduce_scatter | solution.py:53
  873.8 106.6 %reduce-scatter.13.cloned.1.call-done = bf16[32,8192]{1,0:T(8,128)(2,1)} async-done(((bf16[512,8192]{1,0:T(8,128)(2,1)}), bf16[32,8192]{1,0:T(8,128)(2,1)}) %reduce-scatter.13.cloned.1.call-update) | async-done | bytes 524304 | tf_op jit(solution)/shard_map/reduce_scatter | solution.py:53
  980.4 2.3 fusion.51
  982.8 104.5 %reduce-scatter.7.cloned.1.call-done = bf16[32,8192]{1,0:T(8,128)(2,1)} async-done(((bf16[512,8192]{1,0:T(8,128)(2,1)}), bf16[32,8192]{1,0:T(8,128)(2,1)}) %reduce-scatter.7.cloned.1.call-update) | async-done | bytes 524304 | tf_op jit(solution)/shard_map/reduce_scatter | solution.py:53
  1087.2 106.7 %reduce-scatter.9.cloned.1.call-done = bf16[32,8192]{1,0:T(8,128)(2,1)} async-done(((bf16[512,8192]{1,0:T(8,128)(2,1)}), bf16[32,8192]{1,0:T(8,128)(2,1)}) %reduce-scatter.9.cloned.1.call-update) | async-done | bytes 524304 | tf_op jit(solution)/shard_map/reduce_scatter | solution.py:53
  1193.9 2.3 fusion.50
  1198.2 32.2 %psum.7 = f32[]{:T(128)} all-reduce(f32[]{:T(128)S(6)} %add.99), channel_id=1, replica_groups=mesh['rep'=2,'dp'=16] {'dp'}, use_global_device_ids=true, to_apply=%region_12.13 | all-reduce | flops 1 | bytes 8 | tf_op jit(solution)/shard_map/psum | solution.py:55
  1231.1 5.8 fusion.58
  1237.0 0.8 copy-done.11
  1238.0 0.1 copy-done.13
  1238.1 0.1 copy-done.14
  1238.3 0.2 copy-done.15
  1238.4 5.1 fusion.45
  (71 shorter events, 0.9 us)
Async XLA Ops:
  7.2 8.9 copy-start.16
  7.2 9.7 copy-start.17
  7.2 80.9 %all-gather.13.cloned.1.call-start = ((), (), s32[]{:S(2)}) async-start(), calls=%async_computation.12 | async-start | bytes 8912896 | tf_op jit(solution)/shard_map/all_gather | solution.py:40
  9.6 154.0 %all-gather.15.cloned.1.call-start = ((), (), s32[]{:S(2)}) async-start(), calls=%async_computation.13 | async-start | bytes 8912896 | tf_op jit(solution)/shard_map/all_gather | solution.py:40
  11.9 227.2 %all-gather.17.cloned.1.call-start = ((), (), s32[]{:S(2)}) async-start(), calls=%async_computation.14 | async-start | bytes 8912896 | tf_op jit(solution)/shard_map/all_gather | solution.py:40
  14.3 300.3 %all-gather.21.cloned.1.call-start = ((), (), s32[]{:S(2)}) async-start(), calls=%async_computation.16 | async-start | bytes 8912896 | tf_op jit(solution)/shard_map/all_gather | solution.py:40
  14.8 375.1 %all-gather.23.cloned.1.call-start = ((), (), s32[]{:S(2)}) async-start(), calls=%async_computation.17 | async-start | bytes 8912896 | tf_op jit(solution)/shard_map/all_gather | solution.py:40
  15.4 449.8 %all-gather.19.cloned.1.call-start = ((), (), s32[]{:S(2)}) async-start(), calls=%async_computation.15 | async-start | bytes 8912896 | tf_op jit(solution)/shard_map/all_gather | solution.py:40
  16.0 682.9 %reduce-scatter.15.cloned.1.call-start = ((), (), s32[]{:S(2)}) async-start(), calls=%async_computation.10 | async-start | bytes 8912896 | tf_op jit(solution)/shard_map/reduce_scatter | solution.py:53
  16.6 222.5 %copy-start = (bf16[1,1024,512]{1,2,0:T(8,128)(2,1)}, bf16[1,1024,512]{1,2,0:T(8,128)(2,1)S(1)}, u32[]{:S(2)}) copy-start(bf16[1,1024,512]{1,2,0:T(8,128)(2,1)S(1)} %copy.20) | copy-start | bytes 3145732
  16.9 146.7 %copy-start.21 = (f32[1024]{0:T(1024)}, f32[1024]{0:T(1024)S(1)}, u32[]{:S(2)}) copy-start(f32[1024]{0:T(1024)S(1)} %add_rsqrt_fusion) | copy-start | bytes 12292
  254.3 75.4 %copy-start.23 = (f32[1024]{0:T(1024)}, f32[1024]{0:T(1024)S(1)}, u32[]{:S(2)}) copy-start(f32[1024]{0:T(1024)S(1)} %get-tuple-element.26) | copy-start | bytes 12292
  254.3 286.1 %copy-start.5 = (bf16[1024,512]{0,1:T(8,128)(2,1)}, bf16[1024,512]{0,1:T(8,128)(2,1)S(1)}, u32[]{:S(2)}) copy-start(bf16[1024,512]{0,1:T(8,128)(2,1)S(1)} %get-tuple-element.27) | copy-start | bytes 3145732
  254.3 286.1 %copy-start.19 = (f32[1024]{0:T(1024)}, f32[1024]{0:T(1024)S(1)}, u32[]{:S(2)}) copy-start(f32[1024]{0:T(1024)S(1)} %fusion.91) | copy-start | bytes 12292
  506.3 21.1 %copy-start.25 = (bf16[1,512,8192]{2,1,0:T(8,128)(2,1)S(1)}, bf16[1,512,8192]{2,1,0:T(8,128)(2,1)}, u32[]{:S(2)}) copy-start(bf16[1,512,8192]{2,1,0:T(8,128)(2,1)} %all-gather.19.cloned.1.call-done) | copy-start | bytes 25165828
  527.5 12.9 %copy-start.24 = (f32[1024]{0:T(1024)S(1)}, f32[1024]{0:T(1024)}, u32[]{:S(2)}) copy-start(f32[1024]{0:T(1024)} %copy-done.23) | copy-start | bytes 12292
  527.5 12.9 %copy-start.7 = (bf16[1,1024,512]{1,2,0:T(8,128)(2,1)S(1)}, bf16[1,1024,512]{1,2,0:T(8,128)(2,1)}, u32[]{:S(2)}) copy-start(bf16[1,1024,512]{1,2,0:T(8,128)(2,1)} %copy.21) | copy-start | bytes 3145732
  558.5 1.2 copy-start.18
  558.5 208.4 %reduce-scatter.17.cloned.1.call-start = ((), (), s32[]{:S(2)}) async-start(), calls=%async_computation.11 | async-start | bytes 8912896 | tf_op jit(solution)/shard_map/reduce_scatter | solution.py:53
  586.5 16.2 %copy-start.1 = (bf16[1,1024,512]{1,2,0:T(8,128)(2,1)S(1)}, bf16[1,1024,512]{1,2,0:T(8,128)(2,1)}, u32[]{:S(2)}) copy-start(bf16[1,1024,512]{1,2,0:T(8,128)(2,1)} %copy-done) | copy-start | bytes 3145732
  586.5 16.2 %copy-start.22 = (f32[1024]{0:T(1024)S(1)}, f32[1024]{0:T(1024)}, u32[]{:S(2)}) copy-start(f32[1024]{0:T(1024)} %copy-done.21) | copy-start | bytes 12292
  586.6 287.2 %reduce-scatter.11.cloned.1.call-start = ((), (), s32[]{:S(2)}) async-start(), calls=%async_computation.8 | async-start | bytes 8912896 | tf_op jit(solution)/shard_map/reduce_scatter | solution.py:53
  625.0 1.2 copy-start.6
  625.0 1.2 copy-start.20
  625.0 355.4 %reduce-scatter.13.cloned.1.call-start = ((), (), s32[]{:S(2)}) async-start(), calls=%async_computation.9 | async-start | bytes 8912896 | tf_op jit(solution)/shard_map/reduce_scatter | solution.py:53
  648.7 438.5 %reduce-scatter.7.cloned.1.call-start = ((), (), s32[]{:S(2)}) async-start(), calls=%async_computation.6 | async-start | bytes 8912896 | tf_op jit(solution)/shard_map/reduce_scatter | solution.py:53
  681.7 512.2 %reduce-scatter.9.cloned.1.call-start = ((), (), s32[]{:S(2)}) async-start(), calls=%async_computation.7 | async-start | bytes 8912896 | tf_op jit(solution)/shard_map/reduce_scatter | solution.py:53
  698.9 532.2 %copy-start.2 = (bf16[2,512,512]{2,1,0:T(8,128)(2,1)S(1)}, bf16[2,512,512]{2,1,0:T(8,128)(2,1)}, u32[]{:S(2)}) copy-start(bf16[2,512,512]{2,1,0:T(8,128)(2,1)} %param.15) | copy-start | bytes 3145732
  698.9 538.1 %copy-start.3 = (bf16[2,32,8192]{2,1,0:T(8,128)(2,1)S(1)}, bf16[2,32,8192]{2,1,0:T(8,128)(2,1)}, u32[]{:S(2)}) copy-start(bf16[2,32,8192]{2,1,0:T(8,128)(2,1)} %param.13) | copy-start | bytes 3145732
  698.9 538.1 %copy-start.4 = (bf16[2,32,8192]{2,1,0:T(8,128)(2,1)S(1)}, bf16[2,32,8192]{2,1,0:T(8,128)(2,1)}, u32[]{:S(2)}) copy-start(bf16[2,32,8192]{2,1,0:T(8,128)(2,1)} %param.14) | copy-start | bytes 3145732
  1231.0 5.9 copy-start.8
  1231.1 5.9 copy-start.9
  1231.1 5.9 copy-start.10
  1231.1 6.8 copy-start.11
  1231.1 6.9 copy-start.12
  1231.1 7.0 copy-start.13
  1231.1 7.2 copy-start.14
  1231.1 7.3 copy-start.15
Sparse Core Ops, SparseCore 0:
  10.8 77.2 all-gather.12
  90.9 72.6 all-gather.14
  166.4 72.6 all-gather.16
  241.8 72.6 all-gather.20
  317.1 72.6 all-gather.22
  392.5 72.6 all-gather.18
  558.7 101.4 reduce-scatter.14
  664.2 102.7 reduce-scatter.16
  771.0 102.6 reduce-scatter.10
  877.7 102.6 reduce-scatter.12
  984.5 102.6 reduce-scatter.6
  1091.2 102.6 reduce-scatter.8
where the time goes:
time: 1260 us; the launch traced here: 1250 us
  waiting for transfers between devices  838 us (67%)
  matrix products  331 us (26%)
  blocking collectives  32.2 us (3%)
  other arithmetic  19 us (2%)
  between operations  17.7 us (1%)
    reduce_scatter x6, waiting for transfers between devices, step(): lax.psum_scatter(by_w[name], 'dp', scatter_dimension=0, tiled=True)  490 us
    all_gather x6, waiting for transfers between devices, fetched(): lax.all_gather(w[number], 'dp', axis=0, tiled=True)  346 us
    dot_general x5, matrix products, layer(): gate = jnp.dot(a, w['w_gate'], preferred_element_type=jnp.float32)  123 us
    dot_general x5, matrix products, layer(): up = jnp.dot(a, w['w_up'], preferred_element_type=jnp.float32)  118 us
    dot_general x5, matrix products, matmul(): jnp.dot(a, w, preferred_element_type=jnp.float32).astype(jnp.bfloat16)  90.5 us
    psum x1, blocking collectives, step(): squares = lax.psum(sum((jnp.sum(g * g) for g in gradients)), 'dp')  32.2 us
  transfers between devices with their start and end apart: 12, of which 11 were waited for; matrix products, arithmetic and copies ran while one was open for 20% of the time, Pallas kernels for 0%

commit v1 on v0

v1 whole, which is shorter than its diff:
```python
import jax
import jax.numpy as jnp
from jax import lax
from jax.experimental import pallas as pl
from jax.experimental.pallas import tpu as pltpu
from jax.sharding import PartitionSpec as P

F32, BF16 = jnp.float32, jnp.bfloat16
MESH = pl.DeviceIdType.MESH
TOKENS, D, HALF, PART = 1024, 512, 4096, 1024
PAIR, STEP = 2 * TOKENS, 256
MIB = 2**20


def nt(a, b):
    return lax.dot_general(a, b, (((1,), (1,)), ((), ())), preferred_element_type=F32)


def nn(a, b):
    return jnp.dot(a, b, preferred_element_type=F32)


def scaled(wide):
    return lax.rsqrt(jnp.mean(wide * wide, -1, keepdims=True) + 1e-6)


def turned(a):
    return a.astype(F32).T.astype(BF16)


def blocks(body):
    def one(b, _):
        body(pl.ds(pl.multiple_of(b * STEP, STEP), STEP), pl.ds(pl.multiple_of((b * STEP + TOKENS) % PAIR, STEP), STEP))
        return 0

    lax.fori_loop(0, PAIR // STEP, one, 0)


def places():
    me, r = lax.axis_index("dp"), lax.axis_index("rep")
    c, z, y = me % 2, me // 2 % 4, me // 8
    row = [(r, y * 8 + (z + k) % 4 * 2 + c) for k in range(4)]
    return me, r, c, z, y, row, (r, (1 - y) * 8 + z * 2 + c), (r, me // 2 * 2 + 1 - c)


def greet(peers):
    barrier = pltpu.get_barrier_semaphore()
    for peer in peers:
        pl.semaphore_signal(barrier, inc=1, device_id=peer, device_id_type=MESH)
    pl.semaphore_wait(barrier, len(peers))


def remote(src, dst, send_sem, recv_sem, to):
    return pltpu.make_async_remote_copy(src_ref=src, dst_ref=dst, send_sem=send_sem, recv_sem=recv_sem, device_id=to, device_id_type=MESH)


def gather_kernel(
    wt, sd, x, dy, wgu, wd, out_h1, out_a0, out_a1, out_at0, out_at1, out_dy, out_dyt,
    sgu, vg, vu, vd, acc, got, h, a, at, h1, a1, at1, dys, dyt, send_sem, recv_sem, own_sem, load_sem, pair_sem, out_sem,
):
    me, r, c, z, y, row, across, partner = places()
    chip, other = me // 2, (1 - r, me)
    greet(row[1:] + [across, other, partner])

    mine, theirs = pl.ds(0, TOKENS), pl.ds(TOKENS, TOKENS)
    swaps = [(wt.at[1 - c], sgu.at[:, :, c]), (x, h.at[theirs]), (dy, dys.at[theirs])]
    swaps = [remote(src, dst, pair_sem.at[0, i], pair_sem.at[1, i], partner) for i, (src, dst) in enumerate(swaps)]
    stays = [(wt.at[c], sgu.at[:, :, c]), (x, h.at[mine]), (dy, dys.at[mine])]
    stays = [pltpu.make_async_copy(src, dst, load_sem.at[i]) for i, (src, dst) in enumerate(stays)]
    for one in swaps + stays:
        one.start()

    def place(n, i, chip, half):
        ref = wd.at[n, chip] if i == 1 else wgu.at[n, 1 - i // 2, chip]
        return ref if i == 2 else ref.at[half]

    def source(n, i):
        ref = sd.at[n] if i == 1 else sgu.at[n, 1 - i // 2]
        return ref if i == 2 else ref.at[r]

    def origin(slot):
        return (y if slot < 3 else 1 - y) * 4 + (z + (3 if slot < 3 else 7) - slot) % 4

    started = []

    def start(j, src, dst, slot, to):
        one = remote(src, dst, send_sem.at[j * 14 + slot], recv_sem.at[j * 14 + slot], to)
        one.start()
        started.append(one)

    def arrived(j, slot):
        n, i = divmod(j, 3)
        block = place(n, i, origin(slot % 7), 1 - r if slot > 6 else r)
        remote(block, block, send_sem.at[j * 14 + slot], recv_sem.at[j * 14 + slot], other).wait_recv()
        return block

    def begin(j):
        n, i = divmod(j, 3)
        for k in (1, 3, 2):
            start(j, source(n, i), place(n, i, chip, r), k - 1, row[k])

    def own_over_y(j):
        n, i = divmod(j, 3)
        start(j, source(n, i), place(n, i, chip, r), 3, across)

    def relay(j, slot):
        block = arrived(j, slot)
        if slot < 3:
            start(j, block, block, 4 + slot, across)
        if j % 3 < 2:
            start(j, block, block, 7 + slot, other)

    begin(1)
    own_over_y(1)
    swaps[0].wait()
    stays[0].wait()
    owns = []
    for n in range(2):
        for i, (ref, to) in enumerate(((sgu.at[n, 0], wgu.at[n, 0]), (sgu.at[n, 1], wgu.at[n, 1]), (sd.at[n], wd.at[n]))):
            owns.append(pltpu.make_async_copy(ref, to.at[chip], own_sem.at[3 * n + i]))
            owns[-1].start()
    begin(0)
    begin(2)

    saved = []

    def save(src, dst):
        saved.append(pltpu.make_async_copy(src, dst, out_sem.at[len(saved)]))
        saved[-1].start()

    def first_norm():
        for one in swaps[1:] + stays[1:]:
            one.wait()

        def body(rows, _):
            wide = h[rows, :].astype(F32)
            normed = (wide * scaled(wide)).astype(BF16)
            a[rows, :] = normed
            at[:, rows] = turned(normed)
            dyt[:, rows] = turned(dys[rows, :])

        blocks(body)
        save(a, out_a0)
        save(at, out_at0)
        save(dys, out_dy)
        save(dyt, out_dyt)

    def from_row(j):
        for slot in (0, 2, 1):
            relay(j, slot)

    def from_across(j):
        for slot in (3, 4, 6, 5):
            relay(j, slot)

    from_row(1)
    own_over_y(0)
    begin(4)
    first_norm()
    from_row(0)
    from_across(1)
    own_over_y(2)
    begin(3)
    from_row(2)
    begin(5)
    from_across(0)
    own_over_y(4)
    from_across(2)
    for one in owns:
        one.wait()
    for j in (1, 0):
        for slot in range(7, 14):
            arrived(j, slot)
    loads = [(wgu.at[0, 0], vg), (wgu.at[0, 1], vu), (wd.at[0], vd)]
    loads = [pltpu.make_async_copy(src, dst, load_sem.at[i]) for i, (src, dst) in enumerate(loads)]
    for one in loads:
        one.start()
    from_row(4)
    own_over_y(3)
    for one in loads:
        one.wait()

    def forward(t):
        cols = slice(t * D, t * D + D)

        def body(b, _):
            rows = pl.ds(pl.multiple_of(b * D, D), D)
            gate = nn(a[rows, :], vg[:, :, :, cols].reshape(D, D))
            up = nn(a[rows, :], vu[:, :, :, cols].reshape(D, D))
            part = nn((gate * jax.nn.sigmoid(gate) * up).astype(BF16), vd[t].reshape(D, D))
            acc[rows, :] = acc[rows, :] + part if t else part
            return 0

        lax.fori_loop(0, PAIR // D, body, 0)

    later = [lambda: from_row(3), lambda: from_across(4), lambda: own_over_y(5), lambda: from_across(3)]
    for t in range(8):
        forward(t)
        if t % 2:
            later[t // 2]()
    swap = remote(acc, got, pair_sem.at[0, 3], pair_sem.at[1, 3], partner)
    swap.start()
    relay(5, 0)
    swap.wait()

    def second_norm(rows, theirs):
        state = h[rows, :] + (acc[rows, :] + got[theirs, :]).astype(BF16)
        wide = state.astype(F32)
        normed = (wide * scaled(wide)).astype(BF16)
        h1[rows, :] = state
        a1[rows, :] = normed
        at1[:, rows] = turned(normed)

    blocks(second_norm)
    save(h1, out_h1)
    save(a1, out_a1)
    save(at1, out_at1)
    relay(5, 2)
    relay(5, 1)
    from_across(5)
    for j in (4, 3):
        for slot in range(7, 14):
            arrived(j, slot)
    for one in saved:
        one.wait()
    for one in started:
        one.wait_send()


def shape(*dims, dtype=BF16):
    return jax.ShapeDtypeStruct(dims, dtype)


ANY, VMEM = pl.BlockSpec(memory_space=pl.ANY), pl.BlockSpec(memory_space=pltpu.VMEM)


def bf(*dims):
    return pltpu.VMEM(dims, BF16)


def wide(*dims):
    return pltpu.VMEM(dims, F32)


def dma(*dims):
    return pltpu.SemaphoreType.DMA(dims)


def gather(wt, sd, x, dy):
    rows, cols = (PAIR, D), (D, PAIR)
    return pl.pallas_call(
        gather_kernel,
        out_shape=(shape(2, 2, 8, 2, 32, HALF), shape(2, 8, 2, 256, D)) + tuple(shape(*s) for s in (rows, rows, rows, cols, cols, rows, cols)),
        in_specs=[VMEM] * 4,
        out_specs=(ANY,) * 9,
        scratch_shapes=[
            bf(2, 2, 2, 32, HALF), bf(8, 2, 32, HALF), bf(8, 2, 32, HALF), bf(8, 2, 256, D), wide(*rows), wide(*rows),
            bf(*rows), bf(*rows), bf(*cols), bf(*rows), bf(*rows), bf(*cols), bf(*rows), bf(*cols),
            dma(84), dma(84), dma(6), dma(3), dma(2, 4), dma(7),
        ],
        compiler_params=pltpu.CompilerParams(collective_id=0, has_side_effects=True, vmem_limit_bytes=60 * MIB),
        name="gather_forward",
    )(wt, sd, x, dy)


def backward_kernel(
    wgu, wd, a0, a1, at0, at1, dy, dyt, h1, out_d, out_g, square, from_y_d, from_y_g, from_z_d, from_z_g,
    a, at, by_h, by_ht, by_a, got, act, by_gate, by_up, vgu, vd, unit_d, unit_g, stage_yd, stage_yg, sent_d, sent_g, own_d, own_g,
    stage_zd, stage_zg, whole, sums, y_send, y_recv, z_send, z_recv, stage_sem, load_sem, w_sem, pair_sem, core_sem, sum_sem,
):
    me, r, c, z, y, row, across, partner = places()
    greet(row[1:] + [across, partner])

    def trio(d, g):
        return [d, g.at[0], g.at[1]]

    unit, from_y, from_z, stage_y = trio(unit_d, unit_g), trio(from_y_d, from_y_g), trio(from_z_d, from_z_g), trio(stage_yd, stage_yg)
    stage_z, sent, own = trio(stage_zd, stage_zg), trio(sent_d, sent_g), trio(own_d, own_g)

    def over_y(k, i):
        src = unit[i].at[k % 2, pl.ds((1 - y) * 4, 4)]
        return remote(src, from_y[i].at[k], y_send.at[k * 3 + i], y_recv.at[k * 3 + i], across)

    def over_z(k, i, hop):
        at = (k * 3 + i) * 3 + hop - 1
        return remote(sent[i].at[k % 2, hop - 1], from_z[i].at[k, hop - 1], z_send.at[at], z_recv.at[at], row[hop])

    def over_cores(k, i):
        at = (i - 1) * 8 + k
        return remote(whole.at[i - 1, k, 1 - c], out_g.at[i - 1, k, c], core_sem.at[0, at], core_sem.at[1, at], partner)

    def stage_of_y(k, i):
        return pltpu.make_async_copy(from_y[i].at[k], stage_y[i], stage_sem.at[i])

    def stage_of_z(k, i):
        return pltpu.make_async_copy(from_z[i].at[k], stage_z[i], stage_sem.at[3 + i])

    def fetch_y(k, i):
        over_y(k, i).wait_recv()
        stage_of_y(k, i).start()

    def add_y(k, i):
        stage_of_y(k, i).wait()
        over_y(k, i).wait_send()
        for hop in (2, 1, 3, 0):
            to = (z + hop) % 4
            total = unit[i][k % 2, y * 4 + to].astype(F32) + stage_y[i][to].astype(F32)
            if hop:
                sent[i][k % 2, hop - 1] = total.astype(BF16)
                over_z(k, i, hop).start()
            else:
                own[i][k % 2] = total

    def fetch_z(k, i):
        for hop in (1, 3, 2):
            over_z(k, i, hop).wait()
        stage_of_z(k, i).start()

    def add_z(k, i):
        stage_of_z(k, i).wait()
        total = own[i][k % 2]
        for hop in range(3):
            total = total + stage_z[i][hop].astype(F32)
        total = total.astype(BF16)
        if i:
            whole[i - 1, k] = total
            out_g[i - 1, k, c] = whole[i - 1, k, c]
            over_cores(k, i).start()
        else:
            out_d[k] = total
        g = total.astype(F32)
        g = jnp.sum((g * g).reshape(-1, 8, g.shape[-1]), 0)
        parts = [g[:, j : j + 128] for j in range(0, g.shape[-1], 128)]
        sums[0] += sum(parts[1:], parts[0])

    lags = ((add_y, 5), (fetch_y, 4), (add_z, 8), (fetch_z, 7))

    def advance(k, i, known):
        for step, lag in lags:
            back, which = divmod(i - lag, 3)

            @pl.when(known | (k + back >= 0))
            def _():
                step(k + back, which)

    def weights(n, q):
        slot, some = q % 2, pl.ds(pl.multiple_of(q * 128, 128), 128)
        copies = [pltpu.make_async_copy(wd.at[n, :, q // 2, pl.ds(pl.multiple_of(q % 2 * 128, 128), 128)], vd.at[slot], w_sem.at[slot, 8])]
        for j in range(8):
            src = wgu.at[n, :, :, :, :, pl.ds(pl.multiple_of(j * D + q * 128, 128), 128)]
            copies.append(pltpu.make_async_copy(src, vgu.at[slot, :, :, :, :, pl.ds(j * 128, 128)], w_sem.at[slot, j]))
        return copies

    def begin(copies):
        for one in copies:
            one.start()

    def finish(copies):
        for one in copies:
            one.wait()

    def fill(pairs):
        copies = [pltpu.make_async_copy(src, dst, load_sem.at[i]) for i, (src, dst) in enumerate(pairs)]
        begin(copies)
        return copies

    sums[0] = jnp.zeros_like(sums[0])
    loads = fill([(a1, a), (dy, by_h), (at1, at), (dyt, by_ht)])
    begin(weights(1, me * 0))
    finish(loads)

    def layer(n):
        def part(q, _):
            k, slot = (1 - n) * 4 + q, q % 2
            finish(weights(n, q))
            pl.when(q < 3)(lambda: begin(weights(n, q + 1)))
            if n:
                pl.when(q == 3)(lambda: begin(weights(0, q - 3)))

            def body(rows, _):
                gate_w, up_w = (vgu[slot, j].reshape(D, PART) for j in range(2))
                gate, up = nn(a[rows, :], gate_w), nn(a[rows, :], up_w)
                by_act = nt(by_h[rows, :], vd[slot].reshape(PART, D)).astype(BF16).astype(F32)
                sig = jax.nn.sigmoid(gate)
                silu = gate * sig
                act[rows, :] = (silu * up).astype(BF16)
                g = (by_act * up * (sig + silu * (1.0 - sig))).astype(BF16)
                u = (by_act * silu).astype(BF16)
                by_gate[rows, :] = g
                by_up[rows, :] = u
                if n:
                    total = nt(g, gate_w) + nt(u, up_w)

                    @pl.when(q == 0)
                    def _():
                        by_a[rows, :] = total

                    @pl.when(q > 0)
                    def _():
                        by_a[rows, :] += total

            blocks(body)
            for i, (left, right) in enumerate(((by_ht, act), (at, by_gate), (at, by_up))):

                def columns(j, _):
                    cols = pl.ds(pl.multiple_of(j * STEP, STEP), STEP)
                    g = nn(left[...], right[:, cols]).astype(BF16)
                    if i:
                        unit_g[i - 1, k % 2, :, :, :, cols] = g.reshape(8, 2, 32, STEP)
                    else:
                        unit_d[k % 2, 2 * j] = g[:, :128]
                        unit_d[k % 2, 2 * j + 1] = g[:, 128:]
                    return 0

                lax.fori_loop(0, PART // STEP, columns, 0)
                over_y(k, i).start()
                advance(k, i, False)
            return 0

        lax.fori_loop(0, 4, part, 0)

    layer(1)
    swap = remote(by_a, got, pair_sem.at[0], pair_sem.at[1], partner)
    swap.start()
    loads = fill([(a0, a), (at0, at)])
    swap.wait()

    def between(rows, theirs):
        g = (by_a[rows, :] + got[theirs, :]).astype(BF16).astype(F32)
        state = h1[rows, :].astype(F32)
        scale = scaled(state)
        inner = jnp.mean(g * state, -1, keepdims=True)
        total = by_h[rows, :] + (g * scale - state * (scale * scale * scale * inner)).astype(BF16)
        by_h[rows, :] = total
        by_ht[:, rows] = turned(total)

    blocks(between)
    finish(loads)
    layer(0)
    for s in range(24, 32):
        for step, lag in lags:
            if s - lag < 24:
                step(*divmod(s - lag, 3))

    def share(src, at, to):
        one = remote(sums.at[src], sums.at[at], sum_sem.at[0, at], sum_sem.at[1, at], to)
        one.start()
        return one

    share(0, 3, partner).wait()
    sums[1] = sums[0] + sums[3]
    share(1, 4, across).wait()
    sums[2] = sums[1] + sums[4]
    finish([share(2, 4 + hop, row[hop]) for hop in (1, 2, 3)])
    square[...] = sums[2] + sums[5] + sums[6] + sums[7]
    for i in (1, 2):
        for k in range(8):
            over_cores(k, i).wait()


def backward(wgu, wd, a0, a1, at0, at1, dy, dyt, h1):
    rows, cols, g, d = (PAIR, D), (D, PAIR), (2, 32, PART), (D, 128)
    part = (PAIR, PART)
    return pl.pallas_call(
        backward_kernel,
        out_shape=(
            shape(8, *d), shape(2, 8, *g), shape(8, 128, dtype=F32), shape(8, 4, *d), shape(2, 8, 4, *g), shape(8, 3, *d), shape(2, 8, 3, *g),
        ),
        in_specs=[ANY] * 8 + [VMEM],
        out_specs=(VMEM,) * 3 + (ANY,) * 4,
        scratch_shapes=[
            bf(*rows), bf(*cols), bf(*rows), bf(*cols), wide(*rows), wide(*rows), bf(*part), bf(*part), bf(*part),
            bf(2, 2, 8, 2, 32, PART), bf(2, 8, 128, D), bf(2, 8, *d), bf(2, 2, 8, *g), bf(4, *d), bf(2, 4, *g), bf(2, 3, *d), bf(2, 2, 3, *g),
            wide(2, *d), wide(2, 2, *g), bf(3, *d), bf(2, 3, *g), bf(2, 8, *g), wide(8, 8, 128),
            dma(24), dma(24), dma(72), dma(72), dma(6), dma(4), dma(2, 9), dma(2), dma(2, 16), dma(2, 8),
        ],
        compiler_params=pltpu.CompilerParams(collective_id=1, has_side_effects=True, vmem_limit_bytes=63 * MIB),
        name="backward_sum",
    )(wgu, wd, a0, a1, at0, at1, dy, dyt, h1)


def adamw(w, m, v, g):
    m = 0.9 * m + 0.1 * g
    v = 0.95 * v + 0.05 * g * g
    step = m * lax.rsqrt(v + 1e-8) + 0.1 * w
    return (w - 0.02 * step).astype(BF16), m, v


def update_kernel(count, square, by_d, by_gate, by_up, *refs):
    olds, news = refs[:9], refs[9:]
    factor = jnp.minimum(1.0, 0.5 * lax.rsqrt(jnp.sum(square[...]) / count + 1e-30))

    def columns(g):
        pieces = [(j, core, q) for j in range(2) for core in range(2) for q in range(4)]
        return jnp.concatenate([g[0, q, core, :, j * 128 : j * 128 + 128] for j, core, q in pieces], 1)

    for i, g in enumerate((columns(by_gate), columns(by_up), by_d[0].astype(F32).T)):
        w, m, v = (ref[0] for ref in olds[i::3])
        for ref, one in zip(news[i::3], adamw(w.astype(F32), m, v, g.astype(F32) * factor), strict=True):
            ref[0] = one


def update(square, by_d, by_g, arrays):
    grid, layers = (arrays[0].shape[0], 4), arrays[0].shape[0]
    up = pl.BlockSpec((1, 32, 8192 // 4), lambda n, s: (n, 0, s))
    down = pl.BlockSpec((1, 128, D), lambda n, s: (n, s, 0))
    own = [up, up, down] * 3
    g = [pl.BlockSpec((1, 4, 2, 32, STEP), lambda n, s, i=i: (i, 1 - n, 0, 0, s)) for i in range(2)]
    return pl.pallas_call(
        lambda *refs: update_kernel(16 * sum(w.size for w in arrays[:3]), *refs),
        grid=grid,
        out_shape=tuple(jax.ShapeDtypeStruct(w.shape, w.dtype) for w in arrays),
        in_specs=[pl.BlockSpec((8, 128), lambda n, s: (0, 0)), pl.BlockSpec((1, D, 128), lambda n, s: ((1 - n) * 4 + s, 0, 0)), *g, *own],
        out_specs=tuple(own),
        name="update",
    )(square, by_d, by_g, by_g, *arrays)


def solution(mesh):
    def step(x, dy, *arrays):
        w_gate, w_up, w_down = arrays[:3]
        layers = w_gate.shape[0]
        wt = jnp.stack([w_gate, w_up], 1).reshape(layers, 2, 32, 8, 2, D).transpose(4, 0, 1, 2, 3, 5).reshape(2, layers, 2, 32, HALF)
        wgu, wd, h1, *rest = gather(wt, w_down.reshape(layers, 2, 256, D), x[0], dy[0])
        by_d, by_g, square = backward(wgu, wd, *rest, h1)[:3]
        return tuple(update(square, by_d, by_g, arrays))

    states, cut = P(("rep", "dp"), None, None), P(None, "dp", None)
    return jax.shard_map(
        step,
        mesh=mesh,
        in_specs=(states, states) + (cut,) * 9,
        out_specs=(P("rep", "dp", None),) * 9,
        check_vma=False,
    )
```

time: 1260 us -> 612 us (0.49)
  waiting for transfers between devices: 838 us -> 0 us
  Pallas kernels: 0 us -> 605 us
  matrix products: 331 us -> 0 us
  blocking collectives: 32.2 us -> 0 us
  other arithmetic: 19 us -> 0.2 us
  between operations: 17.7 us -> 0.87 us
    pallas_call x0 -> x3, Pallas kernels: none -> 605 us  [the longest x1 358 us: backward(): pl.pallas_call(backward_kernel, out_shape=(shape(8, *d), shape(2, 8, *g),...]
    reduce_scatter x6 -> x0, waiting for transfers between devices: 490 us -> none  [step(): lax.psum_scatter(by_w[name], 'dp', scatter_dimension=0, tiled=True)]
    all_gather x6 -> x0, waiting for transfers between devices: 346 us -> none  [fetched(): lax.all_gather(w[number], 'dp', axis=0, tiled=True)]
    dot_general x15 -> x0, matrix products: 331 us -> none  [the longest x5 123 us: layer(): gate = jnp.dot(a, w['w_gate'], preferred_element_type=jnp.float32)]
    psum x1 -> x0, blocking collectives: 32.2 us -> none  [step(): squares = lax.psum(sum((jnp.sum(g * g) for g in gradients)), 'dp')]
  transfers between devices with their start and end apart: 12 -> 0, of which waited for: 11 -> 0; matrix products, arithmetic and copies ran while one was open for 20% -> 0% of each run, Pallas kernels for 0% -> 0%
where the time goes in v1:
time: 612 us; the launch traced here: 611 us
  Pallas kernels  605 us (99%)
    pallas_call x1, Pallas kernels, backward(): pl.pallas_call(backward_kernel, out_shape=(shape(8, *d), shape(2, 8, *g),...  358 us
    pallas_call x1, Pallas kernels, gather(): pl.pallas_call(gather_kernel, out_shape=(shape(2, 2, 8, 2, 32, HALF), sha...  232 us
    pallas_call x1, Pallas kernels, update(): pl.pallas_call(lambda *refs: update_kernel(16 * sum((w.size for w in arra...  14.6 us

profile of v1, /device:TPU:0, one launch (start us, length us, event | category | flops | bytes accessed | tf_op | source)
XLA Modules:
  0.0 611.3 jit_solution(13881196044005645138)
XLA Ops:
  0.6 0.0 copy-start
  0.7 1.9 stack.9
  2.6 0.2 copy.20
  2.8 0.0 copy-done
  2.8 0.8 stack.10
  3.6 0.2 copy.21
  3.7 0.2 maximum_bitcast_fusion
  4.0 2.3 reshape.29.wt
  6.3 232.3 %gather_forward.1 = (bf16[2,2,8,2,32,4096]{5,4,3,2,1,0:T(8,128)(2,1)}, bf16[2,8,2,256,512]{4,3,2,1,0:T(8,128)(2,1)}, bf16[2048,512]{1,0:T(8,128)(2,1)}, bf16[204...) custom-call(bf16[2,2,2,32,4096]{4,3,2,1,0:T(8,128)(2,1)} %reshape.29, ...), custom_call_target="tpu_custom_call" | custom-call | tf_op jit(solution)/shard_map/gather_forward/pallas_call | solution.py:251
  238.6 358.0 %backward_sum.1 = (bf16[8,512,128]{2,1,0:T(8,128)(2,1)}, bf16[2,8,2,32,1024]{4,3,2,1,0:T(8,128)(2,1)}, f32[8,128]{1,0:T(8,128)}, bf16[8,4,512,128]{3,2,1,0:T(8,1...) custom-call(bf16[2,2,8,2,32,4096]{5,4,3,2,1,0:T(8,128)(2,1)} %get-tu, ...), custom_call_target="tpu_custom_call" | custom-call | tf_op jit(solution)/shard_map/backward_sum/pallas_call | solution.py:464
  596.5 14.6 %update.1 = (bf16[2,32,8192]{2,1,0:T(8,128)(2,1)}, bf16[2,32,8192]{2,1,0:T(8,128)(2,1)}, bf16[2,512,512]{2,1,0:T(8,128)(2,1)}, f32[2,32,8192]{2,1,0:T(8,128)}, f...) custom-call(f32[8,128]{1,0:T(8,128)} %get-tuple-element.30.refs_0_, ...), custom_call_target="tpu_custom_call" | custom-call | tf_op jit(solution)/shard_map/update/pallas_call | solution.py:509
Async XLA Ops:
  0.6 2.1 copy-start

commit v2 on v1

--- a/solution.py
+++ b/solution.py
@@ -28,12 +28,12 @@
     return a.astype(F32).T.astype(BF16)
 
 
-def blocks(body):
+def blocks(body, low=0, high=PAIR // STEP):
     def one(b, _):
         body(pl.ds(pl.multiple_of(b * STEP, STEP), STEP), pl.ds(pl.multiple_of((b * STEP + TOKENS) % PAIR, STEP), STEP))
         return 0
 
-    lax.fori_loop(0, PAIR // STEP, one, 0)
+    lax.fori_loop(low, high, one, 0)
 
 
 def places():
@@ -55,28 +55,43 @@
 
 
 def gather_kernel(
-    wt, sd, x, dy, wgu, wd, out_h1, out_a0, out_a1, out_at0, out_at1, out_dy, out_dyt,
-    sgu, vg, vu, vd, acc, got, h, a, at, h1, a1, at1, dys, dyt, send_sem, recv_sem, own_sem, load_sem, pair_sem, out_sem,
+    w_gate, w_up, sd, x, dy, wgu, wd, out_h1, out_a0, out_a1, out_at0, out_at1, out_dy, out_dyt,
+    give, sgu, vg, vu, vd, acc, got, h, a, at, h1, a1, at1, dys, dyt, send_sem, recv_sem, own_sem, load_sem, pair_sem, out_sem,
 ):
     me, r, c, z, y, row, across, partner = places()
     chip, other = me // 2, (1 - r, me)
+
+    def split(j, _):
+        to, own, its = (pl.ds(pl.multiple_of(at * D, D), D) for at in (j, 2 * j + c, 2 * j + 1 - c))
+        for n in range(2):
+            for m, w in enumerate((w_gate, w_up)):
+                give[n, m, :, to] = w[n, :, its]
+                sgu[n, m, c, :, to] = w[n, :, own]
+        return 0
+
+    lax.fori_loop(0, 8, split, 0)
     greet(row[1:] + [across, other, partner])
 
     mine, theirs = pl.ds(0, TOKENS), pl.ds(TOKENS, TOKENS)
-    swaps = [(wt.at[1 - c], sgu.at[:, :, c]), (x, h.at[theirs]), (dy, dys.at[theirs])]
+    swaps = [(give, sgu.at[:, :, c]), (x, h.at[theirs]), (dy, dys.at[theirs])]
     swaps = [remote(src, dst, pair_sem.at[0, i], pair_sem.at[1, i], partner) for i, (src, dst) in enumerate(swaps)]
-    stays = [(wt.at[c], sgu.at[:, :, c]), (x, h.at[mine]), (dy, dys.at[mine])]
+    stays = [(x, h.at[mine]), (dy, dys.at[mine])]
     stays = [pltpu.make_async_copy(src, dst, load_sem.at[i]) for i, (src, dst) in enumerate(stays)]
     for one in swaps + stays:
         one.start()
 
+    def gate(ref, i):
+        return ref.at[0] if i == 2 else ref.at[1, pl.ds(i * 16 - 48, 16)]
+
     def place(n, i, chip, half):
-        ref = wd.at[n, chip] if i == 1 else wgu.at[n, 1 - i // 2, chip]
-        return ref if i == 2 else ref.at[half]
+        if i > 1:
+            return gate(wgu.at[n, 0, chip], i)
+        return wd.at[n, chip, half] if i else wgu.at[n, 1, chip, half]
 
     def source(n, i):
-        ref = sd.at[n] if i == 1 else sgu.at[n, 1 - i // 2]
-        return ref if i == 2 else ref.at[r]
+        if i > 1:
+            return gate(sgu.at[n, 0], i)
+        return sd.at[n, r] if i else sgu.at[n, 1, r]
 
     def origin(slot):
         return (y if slot < 3 else 1 - y) * 4 + (z + (3 if slot < 3 else 7) - slot) % 4
@@ -89,38 +104,41 @@
         started.append(one)
 
     def arrived(j, slot):
-        n, i = divmod(j, 3)
+        n, i = divmod(j, 5)
         block = place(n, i, origin(slot % 7), 1 - r if slot > 6 else r)
         remote(block, block, send_sem.at[j * 14 + slot], recv_sem.at[j * 14 + slot], other).wait_recv()
         return block
 
     def begin(j):
-        n, i = divmod(j, 3)
+        n, i = divmod(j, 5)
         for k in (1, 3, 2):
             start(j, source(n, i), place(n, i, chip, r), k - 1, row[k])
 
     def own_over_y(j):
-        n, i = divmod(j, 3)
+        n, i = divmod(j, 5)
         start(j, source(n, i), place(n, i, chip, r), 3, across)
+
+    def ahead(j):
+        begin(j)
+        own_over_y(j)
 
     def relay(j, slot):
         block = arrived(j, slot)
         if slot < 3:
             start(j, block, block, 4 + slot, across)
-        if j % 3 < 2:
+        if j % 5 < 2:
             start(j, block, block, 7 + slot, other)
 
-    begin(1)
-    own_over_y(1)
+    ahead(1)
     swaps[0].wait()
-    stays[0].wait()
     owns = []
     for n in range(2):
         for i, (ref, to) in enumerate(((sgu.at[n, 0], wgu.at[n, 0]), (sgu.at[n, 1], wgu.at[n, 1]), (sd.at[n], wd.at[n]))):
             owns.append(pltpu.make_async_copy(ref, to.at[chip], own_sem.at[3 * n + i]))
             owns[-1].start()
-    begin(0)
-    begin(2)
+    ahead(0)
+    for j in (2, 3, 4):
+        own_over_y(j)
 
     saved = []
 
@@ -129,7 +147,7 @@
         saved[-1].start()
 
     def first_norm():
-        for one in swaps[1:] + stays[1:]:
+        for one in swaps[1:] + stays:
             one.wait()
 
         def body(rows, _):
@@ -154,18 +172,21 @@
             relay(j, slot)
 
     from_row(1)
-    own_over_y(0)
-    begin(4)
+    begin(2)
     first_norm()
     from_row(0)
+    begin(3)
+    begin(4)
     from_across(1)
-    own_over_y(2)
-    begin(3)
     from_row(2)
-    begin(5)
+    ahead(6)
     from_across(0)
-    own_over_y(4)
+    from_row(3)
+    from_row(4)
+    ahead(5)
     from_across(2)
+    from_across(3)
+    from_across(4)
     for one in owns:
         one.wait()
     for j in (1, 0):
@@ -175,8 +196,8 @@
     loads = [pltpu.make_async_copy(src, dst, load_sem.at[i]) for i, (src, dst) in enumerate(loads)]
     for one in loads:
         one.start()
-    from_row(4)
-    own_over_y(3)
+    from_row(6)
+    ahead(7)
     for one in loads:
         one.wait()
 
@@ -193,14 +214,15 @@
 
         lax.fori_loop(0, PAIR // D, body, 0)
 
-    later = [lambda: from_row(3), lambda: from_across(4), lambda: own_over_y(5), lambda: from_across(3)]
+    later = {1: (from_row, 5), 2: (ahead, 8), 3: (from_across, 6), 5: (from_across, 5), 6: (from_row, 7)}
     for t in range(8):
         forward(t)
-        if t % 2:
-            later[t // 2]()
+        if t in later:
+            later[t][0](later[t][1])
+    ahead(9)
     swap = remote(acc, got, pair_sem.at[0, 3], pair_sem.at[1, 3], partner)
     swap.start()
-    relay(5, 0)
+    from_across(7)
     swap.wait()
 
     def second_norm(rows, theirs):
@@ -215,10 +237,11 @@
     save(h1, out_h1)
     save(a1, out_a1)
     save(at1, out_at1)
-    relay(5, 2)
-    relay(5, 1)
-    from_across(5)
-    for j in (4, 3):
+    from_row(8)
+    from_row(9)
+    from_across(8)
+    from_across(9)
+    for j in (6, 5):
         for slot in range(7, 14):
             arrived(j, slot)
     for one in saved:
@@ -246,21 +269,21 @@
     return pltpu.SemaphoreType.DMA(dims)
 
 
-def gather(wt, sd, x, dy):
+def gather(*args):
     rows, cols = (PAIR, D), (D, PAIR)
     return pl.pallas_call(
         gather_kernel,
         out_shape=(shape(2, 2, 8, 2, 32, HALF), shape(2, 8, 2, 256, D)) + tuple(shape(*s) for s in (rows, rows, rows, cols, cols, rows, cols)),
-        in_specs=[VMEM] * 4,
+        in_specs=[VMEM] * 5,
         out_specs=(ANY,) * 9,
         scratch_shapes=[
-            bf(2, 2, 2, 32, HALF), bf(8, 2, 32, HALF), bf(8, 2, 32, HALF), bf(8, 2, 256, D), wide(*rows), wide(*rows),
+            bf(2, 2, 32, HALF), bf(2, 2, 2, 32, HALF), bf(8, 2, 32, HALF), bf(8, 2, 32, HALF), bf(8, 2, 256, D), wide(*rows), wide(*rows),
             bf(*rows), bf(*rows), bf(*cols), bf(*rows), bf(*rows), bf(*cols), bf(*rows), bf(*cols),
-            dma(84), dma(84), dma(6), dma(3), dma(2, 4), dma(7),
+            dma(140), dma(140), dma(6), dma(3), dma(2, 4), dma(7),
         ],
         compiler_params=pltpu.CompilerParams(collective_id=0, has_side_effects=True, vmem_limit_bytes=60 * MIB),
         name="gather_forward",
-    )(wt, sd, x, dy)
+    )(*args)
 
 
 def backward_kernel(
@@ -269,7 +292,6 @@
     stage_zd, stage_zg, whole, sums, y_send, y_recv, z_send, z_recv, stage_sem, load_sem, w_sem, pair_sem, core_sem, sum_sem,
 ):
     me, r, c, z, y, row, across, partner = places()
-    greet(row[1:] + [across, partner])
 
     def trio(d, g):
         return [d, g.at[0], g.at[1]]
@@ -333,7 +355,7 @@
         parts = [g[:, j : j + 128] for j in range(0, g.shape[-1], 128)]
         sums[0] += sum(parts[1:], parts[0])
 
-    lags = ((add_y, 5), (fetch_y, 4), (add_z, 8), (fetch_z, 7))
+    lags = ((add_y, 4), (fetch_y, 3), (add_z, 7), (fetch_z, 6))
 
     def advance(k, i, known):
         for step, lag in lags:
@@ -367,6 +389,7 @@
     sums[0] = jnp.zeros_like(sums[0])
     loads = fill([(a1, a), (dy, by_h), (at1, at), (dyt, by_ht)])
     begin(weights(1, me * 0))
+    greet(row[1:] + [across, partner])
     finish(loads)
 
     def layer(n):
@@ -399,7 +422,9 @@
                     def _():
                         by_a[rows, :] += total
 
-            blocks(body)
+            blocks(body, 0, 4)
+            advance(k, 0, False)
+            blocks(body, 4)
             for i, (left, right) in enumerate(((by_ht, act), (at, by_gate), (at, by_up))):
 
                 def columns(j, _):
@@ -414,7 +439,8 @@
 
                 lax.fori_loop(0, PART // STEP, columns, 0)
                 over_y(k, i).start()
-                advance(k, i, False)
+                if i != 1:
+                    advance(k, 1 + i // 2, False)
             return 0
 
         lax.fori_loop(0, 4, part, 0)
@@ -437,7 +463,7 @@
     blocks(between)
     finish(loads)
     layer(0)
-    for s in range(24, 32):
+    for s in range(24, 31):
         for step, lag in lags:
             if s - lag < 24:
                 step(*divmod(s - lag, 3))
@@ -520,8 +546,7 @@
     def step(x, dy, *arrays):
         w_gate, w_up, w_down = arrays[:3]
         layers = w_gate.shape[0]
-        wt = jnp.stack([w_gate, w_up], 1).reshape(layers, 2, 32, 8, 2, D).transpose(4, 0, 1, 2, 3, 5).reshape(2, layers, 2, 32, HALF)
-        wgu, wd, h1, *rest = gather(wt, w_down.reshape(layers, 2, 256, D), x[0], dy[0])
+        wgu, wd, h1, *rest = gather(w_gate, w_up, w_down.reshape(layers, 2, 256, D), x[0], dy[0])
         by_d, by_g, square = backward(wgu, wd, *rest, h1)[:3]
         return tuple(update(square, by_d, by_g, arrays))
 

time: 612 us -> 568 us (0.928)
  Pallas kernels: 605 us -> 567 us
    pallas_call x1, Pallas kernels: 358 us -> 336 us  [backward(): pl.pallas_call(backward_kernel, out_shape=(shape(8, *d), shape(2, 8, *g),...]
    pallas_call x1, Pallas kernels: 232 us -> 216 us  [gather(): pl.pallas_call(gather_kernel, out_shape=(shape(2, 2, 8, 2, 32, HALF), sha...]
where the time goes in v2:
time: 568 us; the launch traced here: 567 us
  Pallas kernels  567 us (100%)
    pallas_call x1, Pallas kernels, backward(): pl.pallas_call(backward_kernel, out_shape=(shape(8, *d), shape(2, 8, *g),...  336 us
    pallas_call x1, Pallas kernels, gather(): pl.pallas_call(gather_kernel, out_shape=(shape(2, 2, 8, 2, 32, HALF), sha...  216 us
    pallas_call x1, Pallas kernels, update(): pl.pallas_call(lambda *refs: update_kernel(16 * sum((w.size for w in arra...  14.6 us

profile of v2, /device:TPU:0, one launch (start us, length us, event | category | flops | bytes accessed | tf_op | source)
XLA Modules:
  0.0 567.4 jit_solution(13398668559367441728)
XLA Ops:
  0.6 216.1 %gather_forward.1 = (bf16[2,2,8,2,32,4096]{5,4,3,2,1,0:T(8,128)(2,1)}, bf16[2,8,2,256,512]{4,3,2,1,0:T(8,128)(2,1)}, bf16[2048,512]{1,0:T(8,128)(2,1)}, bf16[204...) custom-call(bf16[2,32,8192]{2,1,0:T(8,128)(2,1)} %refs_4_.1, ...), custom_call_target="tpu_custom_call" | custom-call | tf_op jit(solution)/shard_map/gather_forward/pallas_call | solution.py:274
  216.8 335.8 %backward_sum.1 = (bf16[8,512,128]{2,1,0:T(8,128)(2,1)}, bf16[2,8,2,32,1024]{4,3,2,1,0:T(8,128)(2,1)}, f32[8,128]{1,0:T(8,128)}, bf16[8,4,512,128]{3,2,1,0:T(8,1...) custom-call(bf16[2,2,8,2,32,4096]{5,4,3,2,1,0:T(8,128)(2,1)} %get-tu, ...), custom_call_target="tpu_custom_call" | custom-call | tf_op jit(solution)/shard_map/backward_sum/pallas_call | solution.py:490
  552.6 14.6 %update.1 = (bf16[2,32,8192]{2,1,0:T(8,128)(2,1)}, bf16[2,32,8192]{2,1,0:T(8,128)(2,1)}, bf16[2,512,512]{2,1,0:T(8,128)(2,1)}, f32[2,32,8192]{2,1,0:T(8,128)}, f...) custom-call(f32[8,128]{1,0:T(8,128)} %get-tuple-element.30.refs_0_, ...), custom_call_target="tpu_custom_call" | custom-call | tf_op jit(solution)/shard_map/update/pallas_call | solution.py:535

commit v3 on v2

--- a/solution.py
+++ b/solution.py
@@ -355,7 +355,7 @@
         parts = [g[:, j : j + 128] for j in range(0, g.shape[-1], 128)]
         sums[0] += sum(parts[1:], parts[0])
 
-    lags = ((add_y, 4), (fetch_y, 3), (add_z, 7), (fetch_z, 6))
+    lags = ((add_y, 4), (fetch_y, 3), (add_z, 8), (fetch_z, 7))
 
     def advance(k, i, known):
         for step, lag in lags:
@@ -463,7 +463,7 @@
     blocks(between)
     finish(loads)
     layer(0)
-    for s in range(24, 31):
+    for s in range(24, 32):
         for step, lag in lags:
             if s - lag < 24:
                 step(*divmod(s - lag, 3))

time: 568 us -> 568 us (level)
  no operation moved by 1% of the time
where the time goes in v3:
time: 568 us; the launch traced here: 567 us
  Pallas kernels  566 us (100%)
    pallas_call x1, Pallas kernels, backward(): pl.pallas_call(backward_kernel, out_shape=(shape(8, *d), shape(2, 8, *g),...  336 us
    pallas_call x1, Pallas kernels, gather(): pl.pallas_call(gather_kernel, out_shape=(shape(2, 2, 8, 2, 32, HALF), sha...  216 us
    pallas_call x1, Pallas kernels, update(): pl.pallas_call(lambda *refs: update_kernel(16 * sum((w.size for w in arra...  14.6 us

profile of v3, /device:TPU:0, one launch (start us, length us, event | category | flops | bytes accessed | tf_op | source)
XLA Modules:
  0.0 567.3 jit_solution(3963339412706731775)
XLA Ops:
  0.6 216.1 %gather_forward.1 = (bf16[2,2,8,2,32,4096]{5,4,3,2,1,0:T(8,128)(2,1)}, bf16[2,8,2,256,512]{4,3,2,1,0:T(8,128)(2,1)}, bf16[2048,512]{1,0:T(8,128)(2,1)}, bf16[204...) custom-call(bf16[2,32,8192]{2,1,0:T(8,128)(2,1)} %refs_4_.1, ...), custom_call_target="tpu_custom_call" | custom-call | tf_op jit(solution)/shard_map/gather_forward/pallas_call | solution.py:274
  216.8 335.7 %backward_sum.1 = (bf16[8,512,128]{2,1,0:T(8,128)(2,1)}, bf16[2,8,2,32,1024]{4,3,2,1,0:T(8,128)(2,1)}, f32[8,128]{1,0:T(8,128)}, bf16[8,4,512,128]{3,2,1,0:T(8,1...) custom-call(bf16[2,2,8,2,32,4096]{5,4,3,2,1,0:T(8,128)(2,1)} %get-tu, ...), custom_call_target="tpu_custom_call" | custom-call | tf_op jit(solution)/shard_map/backward_sum/pallas_call | solution.py:490
  552.5 14.6 %update.1 = (bf16[2,32,8192]{2,1,0:T(8,128)(2,1)}, bf16[2,32,8192]{2,1,0:T(8,128)(2,1)}, bf16[2,512,512]{2,1,0:T(8,128)(2,1)}, f32[2,32,8192]{2,1,0:T(8,128)}, f...) custom-call(f32[8,128]{1,0:T(8,128)} %get-tuple-element.30.refs_0_, ...), custom_call_target="tpu_custom_call" | custom-call | tf_op jit(solution)/shard_map/update/pallas_call | solution.py:535
